TPU v7x, 32 devices: a whole 2x2x4 slice. The times are simulated.
32 devices in a mesh: dom: 32 (over z, y, x, core).
Axes of the slice: x: 2, y: 2, z: 4, core: 2. Of those that a mesh axis runs over, the one named last changes fastest.
Arguments:
- features: bfloat16 [32768, 256], P('dom'), may hold values from -6 to 6
- edge_source: int32 [32, 128, 128], P('dom'), may hold values from 0 to 2047, as said below
- edge_relation: int32 [32, 128, 128], P('dom'), may hold values from 0 to 7
- edge_target: int32 [32, 128, 128], P('dom'), may hold values from 0 to 1023, as said below
- block_count: int32 [32], P('dom'), may hold values from 1 to 128, as said below
- send_list: int32 [32, 32, 32], P('dom'), may hold values from 0 to 1023
- bases_first: bfloat16 [30, 256, 256], P(None, 'dom'), may hold values from -0.375 to 0.375
- self_first: bfloat16 [256, 256], P('dom'), may hold values from -0.375 to 0.375
- coef_first: float32 [8, 30], replicated, may hold values from -1 to 1
- bias_first: float32 [256], replicated, may hold values from -3 to 3
- bases_second: bfloat16 [30, 256, 256], P(None, 'dom'), may hold values from -0.375 to 0.375
- self_second: bfloat16 [256, 256], P('dom'), may hold values from -0.375 to 0.375
- coef_second: float32 [8, 30], replicated, may hold values from -1 to 1
- bias_second: float32 [256], replicated, may hold values from -3 to 3
Outputs:
- embedded: bfloat16 [32768, 256], P('dom')
Inputs may be any that keep to these rules, and one draw needn't show every extreme that they name: `edge_source`: an entry below 1024 names a row of the edge's own partition; an entry 1024 + p * 32 + s names the row that partition p sends to the edge's partition in slot s, and p is never the edge's own partition. `edge_target`: non-decreasing within each block; all targets of one block lie in one aligned window of 16 rows, from 16 * k to 16 * k + 15 for some k. `block_count`: blocks at and beyond it are ignored; some partition uses all 128.
All inputs are finite; a program needn't handle non-finite values.
Results may differ from a plain program's by a relative error of at most 0.0064.
Values may be sent and summed in bfloat16 or wider, within the bound.
A program may use at most 128 MiB of HBM per device.

v0:
```python
import functools

import jax
import jax.numpy as jnp
from jax import lax
from jax.experimental import pallas as pl
from jax.experimental.pallas import tpu as pltpu
from jax.sharding import PartitionSpec as P

WIN = 16
VMEM_LIMIT = 60 * 1024 * 1024


def compose_weights(coef, bases):
    mixed = jnp.einsum(
        "rb,bij->rij", coef, bases.astype(jnp.float32), precision=lax.Precision.HIGHEST
    )
    return mixed.astype(jnp.bfloat16)


def layer_weights(bases, self_weight, coef):
    local_mixed = compose_weights(coef, bases)
    stacked = jnp.concatenate([local_mixed, self_weight[None]], axis=0)
    return lax.all_gather(stacked, "dom", axis=1, tiled=True)


def spread_rows(rows_ref, table_ref, base, parts):
    rows = rows_ref.shape[0]
    step = 256

    def body(chunk, carry):
        first = pl.multiple_of(chunk * step, step)
        for part in range(parts):
            values = rows_ref[pl.ds(first, step), part * 128 : (part + 1) * 128]
            table_ref[pl.ds((base + first) * parts + part, step, stride=parts), :] = values.astype(
                jnp.float32
            )
        return carry

    lax.fori_loop(0, rows // step, body, 0)


def pick_rows(list_ref, major, minor, count, table_ref, held_ref, parts):
    for row in range(count):
        source = list_ref[major, minor + row]
        held_ref[pl.ds(row * parts, parts), :] = table_ref[
            pl.ds(pl.multiple_of(source * parts, parts), parts), :
        ]


def held_rows(held_ref, count, parts):
    return jnp.concatenate(
        [
            held_ref[pl.ds(part, count, stride=parts), :].astype(jnp.bfloat16)
            for part in range(parts)
        ],
        axis=1,
    )


def send_rows_out(send_ref, table_ref, held_a, held_b, out_ref, parts):
    peers, slots = send_ref.shape

    def body(pair, carry):
        for side, held in ((0, held_a), (1, held_b)):
            peer = pair * 2 + side
            pick_rows(send_ref, peer, 0, slots, table_ref, held, parts)
            out_ref[pl.ds(pl.multiple_of(peer * slots, slots), slots), :] = held_rows(
                held, slots, parts
            )
        return carry

    lax.fori_loop(0, peers // 2, body, 0)


def outgoing_kernel(send_ref, rows_ref, out_ref, table_ref, held_a, held_b):
    parts = rows_ref.shape[1] // 128
    spread_rows(rows_ref, table_ref, 0, parts)
    send_rows_out(send_ref, table_ref, held_a, held_b, out_ref, parts)


def layer_kernel(
    last,
    source_ref,
    window_ref,
    count_ref,
    *refs,
):
    if last:
        send_ref = None
        (slot_ref, own_ref, come_ref, weight_ref, bias_ref, out_ref) = refs[:6]
        table_ref, held_a, held_b, pooled_ref, degree_ref = refs[6:]
    else:
        (send_ref, slot_ref, own_ref, come_ref, weight_ref, bias_ref, out_ref, sent_ref) = refs[:8]
        table_ref, held_a, held_b, pooled_ref, degree_ref = refs[8:]
    node_rows, width = own_ref.shape
    parts = width // 128
    tiles, slots, _ = pooled_ref.shape
    relations = slots // WIN
    blocks, block_width = slot_ref.shape
    count = count_ref[0]

    spread_rows(own_ref, table_ref, 0, parts)
    spread_rows(come_ref, table_ref, node_rows, parts)

    def clear(tile, carry):
        pooled_ref[tile] = jnp.zeros(pooled_ref.shape[1:], jnp.float32)
        degree_ref[tile] = jnp.zeros(degree_ref.shape[1:], jnp.float32)
        return carry

    lax.fori_loop(0, tiles, clear, 0)

    slot_ids = lax.broadcasted_iota(jnp.int32, (slots, block_width), 0)
    ones = jnp.ones((block_width, 128), jnp.bfloat16)

    def pool(block, held):
        local = slot_ref[pl.ds(block, 1), :]
        local = jnp.where(block < count, local, -1)
        hot = (slot_ids == local).astype(jnp.float32).astype(jnp.bfloat16)
        sums = jnp.dot(
            hot, held_rows(held, block_width, parts), preferred_element_type=jnp.float32
        )
        numbers = jnp.dot(hot, ones, preferred_element_type=jnp.float32)
        window = window_ref[block]
        pooled_ref[window] += sums
        degree_ref[window] += numbers

    def gather(block, held):
        pick_rows(source_ref, block, 0, block_width, table_ref, held, parts)

    pairs = (count + 1) // 2
    gather(0, held_a)

    def body(pair, carry):
        block = pair * 2
        gather(block + 1, held_b)
        pool(block, held_a)
        gather(jnp.minimum(block + 2, blocks - 1), held_a)
        pool(block + 1, held_b)
        return carry

    lax.fori_loop(0, pairs, body, 0)

    group = 256 // WIN
    bias = bias_ref[...]

    def dense(chunk, carry):
        first = pl.multiple_of(chunk * 256, 256)
        tile = chunk * group
        total = (
            jnp.dot(
                own_ref[pl.ds(first, 256), :],
                weight_ref[relations],
                preferred_element_type=jnp.float32,
            )
            + bias
        )
        for relation in range(relations):
            rows = slice(relation * WIN, (relation + 1) * WIN)
            inverse = 1.0 / jnp.maximum(
                degree_ref[pl.ds(tile, group), rows, :].reshape(256, 128), 1.0
            )
            sums = pooled_ref[pl.ds(tile, group), rows, :].reshape(256, width)
            mean = jnp.concatenate(
                [
                    (sums[:, part * 128 : (part + 1) * 128] * inverse).astype(jnp.bfloat16)
                    for part in range(parts)
                ],
                axis=1,
            )
            total = total + jnp.dot(mean, weight_ref[relation], preferred_element_type=jnp.float32)
        if not last:
            total = jnp.maximum(total, 0.0)
        rounded = total.astype(jnp.bfloat16)
        out_ref[pl.ds(first, 256), :] = rounded
        if not last:
            for part in range(parts):
                table_ref[pl.ds(first * parts + part, 256, stride=parts), :] = rounded[
                    :, part * 128 : (part + 1) * 128
                ].astype(jnp.float32)
        return carry

    lax.fori_loop(0, node_rows // 256, dense, 0)
    if not last:
        send_rows_out(send_ref, table_ref, held_a, held_b, sent_ref, parts)


def in_smem():
    return pl.BlockSpec(memory_space=pltpu.SMEM)


def in_vmem():
    return pl.BlockSpec(memory_space=pltpu.VMEM)


def outgoing_rows(send_rows, rows):
    node_rows, width = rows.shape
    parts = width // 128
    peers, slots = send_rows.shape
    return pl.pallas_call(
        outgoing_kernel,
        out_shape=jax.ShapeDtypeStruct((peers * slots, width), rows.dtype),
        in_specs=[in_smem(), in_vmem()],
        out_specs=in_vmem(),
        scratch_shapes=[
            pltpu.VMEM((node_rows * parts, 128), jnp.float32),
            pltpu.VMEM((slots * parts, 128), jnp.float32),
            pltpu.VMEM((slots * parts, 128), jnp.float32),
        ],
        compiler_params=pltpu.CompilerParams(vmem_limit_bytes=16 * 1024 * 1024),
        name="outgoing",
    )(send_rows, rows)


def relational_layer(last, edges, send_rows, rows, incoming, weights, bias):
    sources, windows, count, local_slot = edges
    node_rows, width = rows.shape
    parts = width // 128
    blocks, block_width = local_slot.shape
    relations = weights.shape[0] - 1
    tiles = node_rows // WIN
    slots = WIN * relations
    table_rows = node_rows + incoming.shape[0]
    result = jax.ShapeDtypeStruct((node_rows, width), rows.dtype)
    if last:
        outs, scalars = result, (sources, windows, count)
    else:
        outs = (result, jax.ShapeDtypeStruct(incoming.shape, rows.dtype))
        scalars = (sources, windows, count, send_rows)
    return pl.pallas_call(
        functools.partial(layer_kernel, last),
        out_shape=outs,
        in_specs=[in_smem()] * len(scalars) + [in_vmem()] * 5,
        out_specs=in_vmem() if last else (in_vmem(), in_vmem()),
        scratch_shapes=[
            pltpu.VMEM((table_rows * parts, 128), jnp.float32),
            pltpu.VMEM((block_width * parts, 128), jnp.float32),
            pltpu.VMEM((block_width * parts, 128), jnp.float32),
            pltpu.VMEM((tiles, slots, width), jnp.float32),
            pltpu.VMEM((tiles, slots, 128), jnp.float32),
        ],
        compiler_params=pltpu.CompilerParams(vmem_limit_bytes=VMEM_LIMIT),
        name="second" if last else "first",
    )(*scalars, local_slot, rows, incoming, weights, bias[None])


def exchange(outgoing, peers):
    slots = outgoing.shape[0] // peers
    shaped = outgoing.reshape(peers, slots, outgoing.shape[1])
    incoming = lax.all_to_all(shaped, "dom", split_axis=0, concat_axis=0, tiled=True)
    return incoming.reshape(outgoing.shape)


def shards(
    features,
    edge_source,
    edge_relation,
    edge_target,
    block_count,
    send_list,
    bases_first,
    self_first,
    coef_first,
    bias_first,
    bases_second,
    self_second,
    coef_second,
    bias_second,
):
    targets = edge_target[0]
    windows = targets[:, 0] // WIN
    local_slot = edge_relation[0] * WIN + targets % WIN
    edges = (edge_source[0], windows, block_count, local_slot)
    send_rows = send_list[0]
    peers = send_rows.shape[0]
    incoming = exchange(outgoing_rows(send_rows, features), peers)
    weights_first = layer_weights(bases_first, self_first, coef_first)
    weights_second = layer_weights(bases_second, self_second, coef_second)
    hidden, outgoing = relational_layer(
        False, edges, send_rows, features, incoming, weights_first, bias_first
    )
    incoming = exchange(outgoing, peers)
    return relational_layer(True, edges, send_rows, hidden, incoming, weights_second, bias_second)


def solution(mesh):
    placed = (
        P("dom", None),
        P("dom", None, None),
        P("dom", None, None),
        P("dom", None, None),
        P("dom"),
        P("dom", None, None),
        P(None, "dom", None),
        P("dom", None),
        P(),
        P(),
        P(None, "dom", None),
        P("dom", None),
        P(),
        P(),
    )
    return jax.shard_map(
        shards, mesh=mesh, in_specs=placed, out_specs=P("dom", None), check_vma=False
    )
```

profile of v0, /device:TPU:0, one launch (start us, length us, event | category | flops | bytes accessed | tf_op | source)
XLA Modules:
  0.0 169.6 jit_solution(8627983411747199482)
XLA Ops:
  6.5 0.0 copy-start
  6.5 0.0 all-gather.3.cloned.1.call-start
  6.5 0.9 copy-done
  7.4 0.9 fusion.2
  8.3 1.3 pad_maximum_fusion
  9.6 0.0 all-gather.3.cloned.1.call-update
  9.6 0.0 all-gather.5.cloned.1.call-start
  9.7 1.1 fusion
  10.8 0.0 copy-start.5
  10.8 0.0 copy-start.6
  10.8 1.3 pad_maximum_fusion.1
  12.2 0.0 all-gather.5.cloned.1.call-update
  12.2 0.0 copy-start.1
  12.2 1.0 copy-done.1
  13.2 0.0 copy-start.2
  13.2 0.7 copy-done.2
  13.9 2.9 %outgoing.1 = bf16[1024,256]{1,0:T(8,128)(2,1)} custom-call(s32[32,32]{1,0:T(8,128)S(1)} %bitcast.21, bf16[1024,256]{1,0:T(8,128)(2,1)S(1)} %copy-done.1), custom_call_target="tpu_custom_call" | custom-call | tf_op jit(solution)/shard_map/outgoing/pallas_call | solution.py:200
  16.8 7.3 %all-to-all-start = ((bf16[32,32,256]{2,1,0:T(8,128)(2,1)}), bf16[32,32,256]{2,1,0:T(8,128)(2,1)S(1)}, u32[]{:S(2)}, u32[]{:S(2)}) async-start(bf16[32,32,256]{2,1,0:T(8,128)(2,1)} %bitcast.4), calls=%async_computation | async-start | bytes 1048576 | tf_op jit(solution)/shard_map/all_to_all | solution.py:250
  24.8 0.0 copy-done.5
  24.8 0.1 slice_reduce_fusion
  24.9 0.5 and_select_fusion.window_ref
  25.5 0.0 copy-done.6
  25.5 0.6 fusion.5.refs_1_.refs_0_
  26.1 14.0 %all-to-all-done = bf16[32,32,256]{2,1,0:T(8,128)(2,1)S(1)} async-done(((bf16[32,32,256]{2,1,0:T(8,128)(2,1)}), bf16[32,32,256]{2,1,0:T(8,128)(2,1)S(1)}, u32[]{:S(2)}, u32[]{:S(2)}) %all-to-all-start) | async-done | bytes 524320 | tf_op jit(solution)/shard_map/all_to_all | solution.py:250
  40.1 0.0 copy-start.4
  40.1 26.2 %all-gather.3.cloned.1.call-done.refs_4_ = bf16[9,256,256]{2,1,0:T(8,128)(2,1)} async-done(((bf16[9,8,256]{2,1,0:T(8,128)(2,1)}), bf16[9,256,256]{2,1,0:T(8,128)(2,1)}) %all-gather.3.cloned.1.call-update) | async-done | bytes 1179664 | tf_op jit(solution)/shard_map/all_gather | solution.py:24
  66.3 0.0 copy-done.4
  66.3 37.2 %first.1 = (bf16[1024,256]{1,0:T(8,128)(2,1)}, bf16[1024,256]{1,0:T(8,128)(2,1)}) custom-call(s32[128,128]{1,0:T(8,128)} %bitcast.25, s32[128]{0:T(128)} %and_select_fusion.window_ref, s32[1]{0:T(128)S(6)} %copy.31.count_ref, s32[32,32]{1,0:T(8,128)} %bitcast.20, s32[128,128]{1,0:T(8,128)} %fusion.5.refs_1_.refs_0_, bf16[1024,256]{1,0:T(8,128)(2,1)} %refs_2_.1, ...), custom_call_target="tpu_custom_call" | custom-call | tf_op jit(solution)/shard_map/first/pallas_call | solution.py:230
  103.5 2.6 %all-to-all-start.1 = ((bf16[32,32,256]{2,1,0:T(8,128)(2,1)}), bf16[32,32,256]{2,1,0:T(8,128)(2,1)S(1)}, u32[]{:S(2)}, u32[]{:S(2)}) async-start(bf16[32,32,256]{2,1,0:T(8,128)(2,1)} %bitcast.24), calls=%async_computation.1 | async-start | bytes 1048576 | tf_op jit(solution)/shard_map/all_to_all | solution.py:250
  106.1 20.2 %all-gather.5.cloned.1.call-done.refs_3_ = bf16[9,256,256]{2,1,0:T(8,128)(2,1)} async-done(((bf16[9,8,256]{2,1,0:T(8,128)(2,1)}), bf16[9,256,256]{2,1,0:T(8,128)(2,1)}) %all-gather.5.cloned.1.call-update) | async-done | bytes 1179664 | tf_op jit(solution)/shard_map/all_gather | solution.py:24
  126.3 0.2 all-to-all-done.1
  126.5 0.0 copy-start.3
  126.5 0.8 copy-done.3
  127.3 35.5 %second.1 = bf16[1024,256]{1,0:T(8,128)(2,1)} custom-call(s32[128,128]{1,0:T(8,128)} %bitcast.26, s32[128]{0:T(128)} %and_select_fusion.window_ref, s32[1]{0:T(128)S(6)} %copy.31.count_ref, s32[128,128]{1,0:T(8,128)} %fusion.5.refs_1_.refs_0_, bf16[1024,256]{1,0:T(8,128)(2,1)} %get-tuple-element.7.refs_1_, bf16[1024,256]{1,0:T(8,128)(2,1)} %bitcast.22, ...), custom_call_target="tpu_custom_call" | custom-call | tf_op jit(solution)/shard_map/second/pallas_call | solution.py:230
  (2 shorter events, 0.0 us)
Async XLA Ops:
  6.5 0.9 copy-start
  6.5 59.8 %all-gather.3.cloned.1.call-start = ((), (), s32[]{:S(2)}) async-start(), calls=%async_computation.2 | async-start | bytes 1216512 | tf_op jit(solution)/shard_map/all_gather | solution.py:24
  9.6 116.6 %all-gather.5.cloned.1.call-start = ((), (), s32[]{:S(2)}) async-start(), calls=%async_computation.3 | async-start | bytes 1216512 | tf_op jit(solution)/shard_map/all_gather | solution.py:24
  10.8 14.0 %copy-start.5 = (s32[1,128,128]{2,1,0:T(8,128)S(1)}, s32[1,128,128]{2,1,0:T(8,128)}, u32[]{:S(2)}) copy-start(s32[1,128,128]{2,1,0:T(8,128)} %param.17) | copy-start | bytes 196612
  10.8 14.7 %copy-start.6 = (s32[1,128,128]{2,1,0:T(8,128)S(1)}, s32[1,128,128]{2,1,0:T(8,128)}, u32[]{:S(2)}) copy-start(s32[1,128,128]{2,1,0:T(8,128)} %param.16) | copy-start | bytes 196612
  12.2 1.0 copy-start.1
  13.2 0.7 copy-start.2
  16.8 23.3 %all-to-all-start = ((bf16[32,32,256]{2,1,0:T(8,128)(2,1)}), bf16[32,32,256]{2,1,0:T(8,128)(2,1)S(1)}, u32[]{:S(2)}, u32[]{:S(2)}) async-start(bf16[32,32,256]{2,1,0:T(8,128)(2,1)} %bitcast.4), calls=%async_computation | async-start | bytes 1048576 | tf_op jit(solution)/shard_map/all_to_all | solution.py:250
  40.1 26.2 %copy-start.4 = (bf16[32,32,256]{2,1,0:T(8,128)(2,1)}, bf16[32,32,256]{2,1,0:T(8,128)(2,1)S(1)}, u32[]{:S(2)}) copy-start(bf16[32,32,256]{2,1,0:T(8,128)(2,1)S(1)} %all-to-all-done) | copy-start | bytes 1572868
  103.5 23.0 %all-to-all-start.1 = ((bf16[32,32,256]{2,1,0:T(8,128)(2,1)}), bf16[32,32,256]{2,1,0:T(8,128)(2,1)S(1)}, u32[]{:S(2)}, u32[]{:S(2)}) async-start(bf16[32,32,256]{2,1,0:T(8,128)(2,1)} %bitcast.24), calls=%async_computation.1 | async-start | bytes 1048576 | tf_op jit(solution)/shard_map/all_to_all | solution.py:250
  126.5 0.8 copy-start.3
Sparse Core Ops, SparseCore 0:
  10.2 56.0 all-gather.2
  69.2 57.0 all-gather.4
where the time goes:
time: 170 us
  Pallas kernels  75.5 us (44%)
  waiting for transfers between devices  60.6 us (36%)
  between operations  14.1 us (8%)
  starting transfers between devices  9.97 us (6%)
  other arithmetic  3.8 us (2%)
  local copies, waits for them, and re-layouts  3.59 us (2%)
  matrix products  1.95 us (1%)
    pallas_call x2, Pallas kernels, relational_layer(): pl.pallas_call(functools.partial(layer_kernel, last), out_shape=outs, in_...  72.7 us
    all_gather x2, waiting for transfers between devices, layer_weights(): return lax.all_gather(stacked, 'dom', axis=1, tiled=True)  46.4 us
    all_to_all x2, waiting for transfers between devices, exchange(): lax.all_to_all(shaped, 'dom', split_axis=0, concat_axis=0, tiled=True)  14.2 us
    all_to_all x2, starting transfers between devices, exchange(): lax.all_to_all(shaped, 'dom', split_axis=0, concat_axis=0, tiled=True)  9.93 us
    unnamed x14, local copies, waits for them, and re-layouts  3.47 us
  transfers between devices with their start and end apart: 4, of which 4 were waited for; matrix products, arithmetic and copies ran while one was open for 2% of the time, Pallas kernels for 24%

commit v1 on v0

--- a/solution.py
+++ b/solution.py
@@ -1,4 +1,5 @@
 import functools
+import math
 
 import jax
 import jax.numpy as jnp
@@ -8,7 +9,7 @@
 from jax.sharding import PartitionSpec as P
 
 WIN = 16
-VMEM_LIMIT = 60 * 1024 * 1024
+VMEM_LIMIT = 40 * 1024 * 1024
 
 
 def compose_weights(coef, bases):
@@ -18,10 +19,57 @@
     return mixed.astype(jnp.bfloat16)
 
 
-def layer_weights(bases, self_weight, coef):
+def weight_share(bases, self_weight, coef):
     local_mixed = compose_weights(coef, bases)
-    stacked = jnp.concatenate([local_mixed, self_weight[None]], axis=0)
-    return lax.all_gather(stacked, "dom", axis=1, tiled=True)
+    return jnp.concatenate([local_mixed, self_weight[None]], axis=0)[:, None]
+
+
+def digits_of(devices):
+    chips = devices // 2
+    side = max(math.isqrt(chips // 4), 1)
+    sizes = (side, side, chips // (side * side))
+    digits, stride = [], 2
+    for size in sizes:
+        digits.append((size, stride))
+        stride *= size
+    return digits
+
+
+def shift_pairs(devices, radix, stride, hop):
+    pairs = []
+    for device in range(devices):
+        digit = device // stride % radix
+        pairs.append((device, device + ((digit + hop) % radix - digit) * stride))
+    return pairs
+
+
+def send_digit(share, devices, radix, stride):
+    return [
+        lax.ppermute(share, "dom", shift_pairs(devices, radix, stride, hop))
+        for hop in range(1, radix)
+    ]
+
+
+def join_digit(share, came, radix, stride, inner=False):
+    if radix == 1:
+        return share
+    digit = lax.axis_index("dom") // stride % radix
+    place = 2 if inner else 1
+    if radix == 2:
+        low = digit == 0
+        parts = [jnp.where(low, share, came[0]), jnp.where(low, came[0], share)]
+        full = jnp.stack(parts, axis=place)
+    else:
+        full = jnp.stack([share] * radix, axis=place)
+        for hop, piece in enumerate(came, start=1):
+            start = [0] * full.ndim
+            start[place] = lax.rem(digit + radix - hop, radix)
+            full = lax.dynamic_update_slice(full, jnp.expand_dims(piece, place), start)
+    return full.reshape(share.shape[0], share.shape[1] * radix, *share.shape[2:])
+
+
+def gather_digit(share, devices, radix, stride, inner=False):
+    return join_digit(share, send_digit(share, devices, radix, stride), radix, stride, inner)
 
 
 def spread_rows(rows_ref, table_ref, base, parts):
@@ -79,20 +127,20 @@
     send_rows_out(send_ref, table_ref, held_a, held_b, out_ref, parts)
 
 
-def layer_kernel(
-    last,
+def pool_kernel(
     source_ref,
     window_ref,
     count_ref,
-    *refs,
+    slot_ref,
+    own_ref,
+    come_ref,
+    mean_ref,
+    table_ref,
+    held_a,
+    held_b,
+    pooled_ref,
+    degree_ref,
 ):
-    if last:
-        send_ref = None
-        (slot_ref, own_ref, come_ref, weight_ref, bias_ref, out_ref) = refs[:6]
-        table_ref, held_a, held_b, pooled_ref, degree_ref = refs[6:]
-    else:
-        (send_ref, slot_ref, own_ref, come_ref, weight_ref, bias_ref, out_ref, sent_ref) = refs[:8]
-        table_ref, held_a, held_b, pooled_ref, degree_ref = refs[8:]
     node_rows, width = own_ref.shape
     parts = width // 128
     tiles, slots, _ = pooled_ref.shape
@@ -126,56 +174,65 @@
         degree_ref[window] += numbers
 
     def gather(block, held):
+        block = jnp.minimum(block, blocks - 1)
         pick_rows(source_ref, block, 0, block_width, table_ref, held, parts)
 
-    pairs = (count + 1) // 2
     gather(0, held_a)
 
     def body(pair, carry):
         block = pair * 2
         gather(block + 1, held_b)
         pool(block, held_a)
-        gather(jnp.minimum(block + 2, blocks - 1), held_a)
-        pool(block + 1, held_b)
-        return carry
-
-    lax.fori_loop(0, pairs, body, 0)
-
-    group = 256 // WIN
+        gather(block + 2, held_a)
+        pool(jnp.minimum(block + 1, blocks - 1), held_b)
+        return carry
+
+    lax.fori_loop(0, (count + 1) // 2, body, 0)
+
+    def average(tile, carry):
+        first = pl.multiple_of(tile * WIN, WIN)
+        for relation in range(relations):
+            rows = slice(relation * WIN, (relation + 1) * WIN)
+            inverse = 1.0 / jnp.maximum(degree_ref[tile, rows, :], 1.0)
+            for part in range(parts):
+                lanes = slice(part * 128, (part + 1) * 128)
+                mean_ref[relation, pl.ds(first, WIN), lanes] = (
+                    pooled_ref[tile, rows, lanes] * inverse
+                ).astype(jnp.bfloat16)
+        return carry
+
+    lax.fori_loop(0, tiles, average, 0)
+
+
+def dense_kernel(last, *refs):
+    if last:
+        own_ref, mean_ref, weight_ref, bias_ref, out_ref = refs
+    else:
+        send_ref, own_ref, mean_ref, weight_ref, bias_ref, out_ref, sent_ref = refs[:7]
+        table_ref, held_a, held_b = refs[7:]
+    node_rows, width = own_ref.shape
+    parts = width // 128
+    relations = mean_ref.shape[0]
     bias = bias_ref[...]
 
     def dense(chunk, carry):
-        first = pl.multiple_of(chunk * 256, 256)
-        tile = chunk * group
-        total = (
-            jnp.dot(
-                own_ref[pl.ds(first, 256), :],
-                weight_ref[relations],
+        rows = pl.ds(pl.multiple_of(chunk * 256, 256), 256)
+        total = bias + jnp.dot(
+            own_ref[rows, :], weight_ref[relations], preferred_element_type=jnp.float32
+        )
+        for relation in range(relations):
+            total = total + jnp.dot(
+                mean_ref[relation, rows, :],
+                weight_ref[relation],
                 preferred_element_type=jnp.float32,
             )
-            + bias
-        )
-        for relation in range(relations):
-            rows = slice(relation * WIN, (relation + 1) * WIN)
-            inverse = 1.0 / jnp.maximum(
-                degree_ref[pl.ds(tile, group), rows, :].reshape(256, 128), 1.0
-            )
-            sums = pooled_ref[pl.ds(tile, group), rows, :].reshape(256, width)
-            mean = jnp.concatenate(
-                [
-                    (sums[:, part * 128 : (part + 1) * 128] * inverse).astype(jnp.bfloat16)
-                    for part in range(parts)
-                ],
-                axis=1,
-            )
-            total = total + jnp.dot(mean, weight_ref[relation], preferred_element_type=jnp.float32)
         if not last:
             total = jnp.maximum(total, 0.0)
         rounded = total.astype(jnp.bfloat16)
-        out_ref[pl.ds(first, 256), :] = rounded
+        out_ref[rows, :] = rounded
         if not last:
             for part in range(parts):
-                table_ref[pl.ds(first * parts + part, 256, stride=parts), :] = rounded[
+                table_ref[pl.ds(chunk * 256 * parts + part, 256, stride=parts), :] = rounded[
                     :, part * 128 : (part + 1) * 128
                 ].astype(jnp.float32)
         return carry
@@ -183,6 +240,45 @@
     lax.fori_loop(0, node_rows // 256, dense, 0)
     if not last:
         send_rows_out(send_ref, table_ref, held_a, held_b, sent_ref, parts)
+
+
+def exchange_kernel(devices, out_ref, in_ref, send_sems, recv_sems):
+    me = lax.axis_index("dom")
+
+    def copy_to(hop):
+        peer = lax.rem(me + hop, devices)
+        return pltpu.make_async_remote_copy(
+            src_ref=out_ref.at[peer],
+            dst_ref=in_ref.at[me],
+            send_sem=send_sems.at[hop],
+            recv_sem=recv_sems.at[hop],
+            device_id=(peer,),
+            device_id_type=pl.DeviceIdType.MESH,
+        )
+
+    def copy_from(hop):
+        peer = lax.rem(me + devices - hop, devices)
+        return pltpu.make_async_remote_copy(
+            src_ref=out_ref.at[peer],
+            dst_ref=in_ref.at[peer],
+            send_sem=send_sems.at[hop],
+            recv_sem=recv_sems.at[hop],
+            device_id=(peer,),
+            device_id_type=pl.DeviceIdType.MESH,
+        )
+
+    def start(hop, carry):
+        copy_to(hop).start()
+        return carry
+
+    def finish(hop, carry):
+        copy_to(hop).wait_send()
+        copy_from(hop).wait_recv()
+        return carry
+
+    lax.fori_loop(1, devices, start, 0)
+    in_ref[me] = out_ref[me]
+    lax.fori_loop(1, devices, finish, 0)
 
 
 def in_smem():
@@ -212,26 +308,19 @@
     )(send_rows, rows)
 
 
-def relational_layer(last, edges, send_rows, rows, incoming, weights, bias):
+def pooled_means(name, edges, rows, incoming, relations):
     sources, windows, count, local_slot = edges
     node_rows, width = rows.shape
     parts = width // 128
-    blocks, block_width = local_slot.shape
-    relations = weights.shape[0] - 1
+    block_width = local_slot.shape[1]
     tiles = node_rows // WIN
     slots = WIN * relations
     table_rows = node_rows + incoming.shape[0]
-    result = jax.ShapeDtypeStruct((node_rows, width), rows.dtype)
-    if last:
-        outs, scalars = result, (sources, windows, count)
-    else:
-        outs = (result, jax.ShapeDtypeStruct(incoming.shape, rows.dtype))
-        scalars = (sources, windows, count, send_rows)
     return pl.pallas_call(
-        functools.partial(layer_kernel, last),
-        out_shape=outs,
-        in_specs=[in_smem()] * len(scalars) + [in_vmem()] * 5,
-        out_specs=in_vmem() if last else (in_vmem(), in_vmem()),
+        pool_kernel,
+        out_shape=jax.ShapeDtypeStruct((relations, node_rows, width), jnp.bfloat16),
+        in_specs=[in_smem()] * 3 + [in_vmem()] * 3,
+        out_specs=in_vmem(),
         scratch_shapes=[
             pltpu.VMEM((table_rows * parts, 128), jnp.float32),
             pltpu.VMEM((block_width * parts, 128), jnp.float32),
@@ -240,14 +329,62 @@
             pltpu.VMEM((tiles, slots, 128), jnp.float32),
         ],
         compiler_params=pltpu.CompilerParams(vmem_limit_bytes=VMEM_LIMIT),
-        name="second" if last else "first",
-    )(*scalars, local_slot, rows, incoming, weights, bias[None])
+        cost_estimate=pl.CostEstimate(
+            flops=20_000_000_000, bytes_accessed=4_000_000, transcendentals=0
+        ),
+        name=name,
+    )(sources, windows, count, local_slot, rows, incoming)
+
+
+def dense_rows(name, send_rows, rows, means, weights, bias):
+    node_rows, width = rows.shape
+    parts = width // 128
+    last = send_rows is None
+    result = jax.ShapeDtypeStruct((node_rows, width), rows.dtype)
+    scratch = []
+    if not last:
+        peers, slots = send_rows.shape
+        scratch = [
+            pltpu.VMEM((node_rows * parts, 128), jnp.float32),
+            pltpu.VMEM((slots * parts, 128), jnp.float32),
+            pltpu.VMEM((slots * parts, 128), jnp.float32),
+        ]
+    return pl.pallas_call(
+        functools.partial(dense_kernel, last),
+        out_shape=result
+        if last
+        else (result, jax.ShapeDtypeStruct((peers * slots, width), rows.dtype)),
+        in_specs=[in_smem()] * (not last) + [in_vmem()] * 4,
+        out_specs=in_vmem() if last else (in_vmem(), in_vmem()),
+        scratch_shapes=scratch,
+        compiler_params=pltpu.CompilerParams(vmem_limit_bytes=24 * 1024 * 1024),
+        cost_estimate=pl.CostEstimate(
+            flops=3_000_000_000, bytes_accessed=6_000_000, transcendentals=0
+        ),
+        name=name,
+    )(*([] if last else [send_rows]), rows, means, weights, bias[None])
 
 
 def exchange(outgoing, peers):
     slots = outgoing.shape[0] // peers
     shaped = outgoing.reshape(peers, slots, outgoing.shape[1])
-    incoming = lax.all_to_all(shaped, "dom", split_axis=0, concat_axis=0, tiled=True)
+    incoming = pl.pallas_call(
+        functools.partial(exchange_kernel, peers),
+        out_shape=jax.ShapeDtypeStruct(shaped.shape, shaped.dtype),
+        in_specs=[in_vmem()],
+        out_specs=in_vmem(),
+        scratch_shapes=[
+            pltpu.SemaphoreType.DMA((peers,)),
+            pltpu.SemaphoreType.DMA((peers,)),
+        ],
+        compiler_params=pltpu.CompilerParams(
+            has_side_effects=True, vmem_limit_bytes=16 * 1024 * 1024
+        ),
+        cost_estimate=pl.CostEstimate(
+            flops=10_000_000_000, bytes_accessed=1_000_000, transcendentals=0
+        ),
+        name="exchange",
+    )(shaped)
     return incoming.reshape(outgoing.shape)
 
 
@@ -273,14 +410,46 @@
     edges = (edge_source[0], windows, block_count, local_slot)
     send_rows = send_list[0]
     peers = send_rows.shape[0]
-    incoming = exchange(outgoing_rows(send_rows, features), peers)
-    weights_first = layer_weights(bases_first, self_first, coef_first)
-    weights_second = layer_weights(bases_second, self_second, coef_second)
-    hidden, outgoing = relational_layer(
-        False, edges, send_rows, features, incoming, weights_first, bias_first
+    relations = coef_first.shape[0]
+    width = features.shape[1]
+    digits = digits_of(peers)
+    share_first = weight_share(bases_first, self_first, coef_first)
+    share_second = weight_share(bases_second, self_second, coef_second)
+
+    along_x, along_y, along_z = digits
+
+    early = jnp.concatenate([share_first, share_second], axis=0)
+    early = gather_digit(early, peers, *along_x)
+    share_first, share_second = early[: relations + 1], early[relations + 1 :]
+    share_first = gather_digit(share_first, peers, *along_y)
+    outgoing = outgoing_rows(send_rows, features)
+    outgoing, share_first, share_second = lax.optimization_barrier(
+        (outgoing, share_first, share_second)
     )
     incoming = exchange(outgoing, peers)
-    return relational_layer(True, edges, send_rows, hidden, incoming, weights_second, bias_second)
+    incoming, share_first, share_second = lax.optimization_barrier(
+        (incoming, share_first, share_second)
+    )
+    came_second = send_digit(share_second, peers, *along_y)
+    came_first = send_digit(share_first, peers, *along_z)
+    means = pooled_means("pool_first", edges, features, incoming, relations)
+    means, came_first, came_second = lax.optimization_barrier((means, came_first, came_second))
+    share_first = gather_digit(join_digit(share_first, came_first, *along_z), peers, 2, 1, True)
+    share_second = join_digit(share_second, came_second, *along_y)
+    weights_first = share_first.reshape(relations + 1, width, width)
+    hidden, outgoing = dense_rows(
+        "dense_first", send_rows, features, means, weights_first, bias_first
+    )
+    incoming = exchange(outgoing, peers)
+    incoming, share_second = lax.optimization_barrier((incoming, share_second))
+    came_second = send_digit(share_second, peers, *along_z)
+    means = pooled_means("pool_second", edges, hidden, incoming, relations)
+    means, came_second = lax.optimization_barrier((means, came_second))
+    share_second = gather_digit(
+        join_digit(share_second, came_second, *along_z), peers, 2, 1, True
+    )
+    weights_second = share_second.reshape(relations + 1, width, width)
+    return dense_rows("dense_second", None, hidden, means, weights_second, bias_second)
 
 
 def solution(mesh):

time: 170 us -> 147 us (0.86)
  waiting for transfers between devices: 60.6 us -> 7.31 us
  Pallas kernels: 75.5 us -> 103 us
  between operations: 14.1 us -> 1.14 us
  starting transfers between devices: 9.97 us -> 22.5 us
  local copies, waits for them, and re-layouts: 3.59 us -> 7.53 us
  other arithmetic: 3.8 us -> 1.68 us
    all_gather x2 -> x0, waiting for transfers between devices: 46.4 us -> none  [layer_weights(): return lax.all_gather(stacked, 'dom', axis=1, tiled=True)]
    pallas_call x2 -> x6, Pallas kernels: 72.7 us -> 101 us  [the longest x2 64.9 us: pooled_means(): pl.pallas_call(pool_kernel, out_shape=jax.ShapeDtypeStruct((relations, no...]
    ppermute x0 -> x11, starting transfers between devices: none -> 22.5 us  [send_digit(): lax.ppermute(share, 'dom', shift_pairs(devices, radix, stride, hop))]
    all_to_all x2 -> x0, waiting for transfers between devices: 14.2 us -> none  [exchange(): lax.all_to_all(shaped, 'dom', split_axis=0, concat_axis=0, tiled=True)]
    all_to_all x2 -> x0, starting transfers between devices: 9.93 us -> none  [exchange(): lax.all_to_all(shaped, 'dom', split_axis=0, concat_axis=0, tiled=True)]
    ppermute x0 -> x11, waiting for transfers between devices: none -> 7.31 us  [send_digit(): lax.ppermute(share, 'dom', shift_pairs(devices, radix, stride, hop))]
    concatenate x2 -> x1, other arithmetic: 2.62 us -> 0.03 us  [shards(): early = jnp.concatenate([share_first, share_second], axis=0)]
    unnamed x14 -> x16, local copies, waits for them, and re-layouts: 3.47 us -> 4.46 us
  transfers between devices with their start and end apart: 4 -> 11, of which waited for: 4 -> 3; matrix products, arithmetic and copies ran while one was open for 2% -> 1% of each run, Pallas kernels for 24% -> 46%
where the time goes in v1:
time: 147 us; the launch traced here: 145 us
  Pallas kernels  103 us (70%)
  starting transfers between devices  22.5 us (15%)
  local copies, waits for them, and re-layouts  7.53 us (5%)
  waiting for transfers between devices  7.31 us (5%)
  matrix products  1.95 us (1%)
  other arithmetic  1.68 us (1%)
    pallas_call x2, Pallas kernels, pooled_means(): pl.pallas_call(pool_kernel, out_shape=jax.ShapeDtypeStruct((relations, no...  64.9 us
    pallas_call x2, Pallas kernels, exchange(): pl.pallas_call(functools.partial(exchange_kernel, peers), out_shape=jax.S...  29.4 us
    ppermute x11, starting transfers between devices, send_digit(): lax.ppermute(share, 'dom', shift_pairs(devices, radix, stride, hop))  22.5 us
    ppermute x11, waiting for transfers between devices, send_digit(): lax.ppermute(share, 'dom', shift_pairs(devices, radix, stride, hop))  7.31 us
    pallas_call x2, Pallas kernels, dense_rows(): pl.pallas_call(functools.partial(dense_kernel, last), out_shape=result if...  6.67 us
    unnamed x16, local copies, waits for them, and re-layouts  4.46 us
  transfers between devices with their start and end apart: 11, of which 3 were waited for; matrix products, arithmetic and copies ran while one was open for 1% of the time, Pallas kernels for 46%

profile of v1, /device:TPU:0, one launch (start us, length us, event | category | flops | bytes accessed | tf_op | source)
XLA Modules:
  0.0 145.3 jit_solution(3497807924960170379)
XLA Ops:
  0.0 0.8 copy.29
  0.8 0.7 copy.31
  1.5 0.9 convolution_convert_fusion.1
  2.3 1.1 convolution_convert_fusion
  3.5 3.0 %collective-permute-start = (bf16[18,1,8,256]{3,0,2,1:T(8,128)(2,1)S(1)}, bf16[18,1,8,256]{3,0,2,1:T(8,128)(2,1)S(1)}, u32[]{:S(2)}, u32[]{:S(2)}) collective-permute-start(bf16[18,1,8,256]{3,0,2,1:T(8,128)(2,1)S(1)} %pad_maximum_fusion.5), channel_id=1, source_target_pairs={{0,2},{1,3},{2,0},{3,1},{4,6},{5,7},{6,4},{7,5},{8,10},{9,11},{10,... | collective-permute-start | bytes 221192 | tf_op jit(solution)/shard_map/ppermute | solution.py:48
  6.5 0.9 slice_reduce_fusion
  7.5 0.9 fusion.6.slot_ref
  9.2 2.1 %outgoing.1 = bf16[1024,256]{1,0:T(8,128)(2,1)S(1)} custom-call(s32[32,32]{1,0:T(8,128)S(1)} %bitcast.71, bf16[1024,256]{1,0:T(8,128)(2,1)S(1)} %copy-done.1), custom_call_target="tpu_custom_call" | custom-call | tf_op jit(solution)/shard_map/outgoing/pallas_call | solution.py:296
  11.3 0.1 select_bitcast_fusion.9
  11.4 1.6 %collective-permute-start.1 = (bf16[9,2,8,256]{3,0,2,1:T(8,128)(2,1)S(1)}, bf16[9,2,8,256]{3,0,2,1:T(8,128)(2,1)S(1)}, u32[]{:S(2)}, u32[]{:S(2)}) collective-permute-start(bf16[9,2,8,256]{3,0,2,1:T(8,128)(2,1)S(1)} %slice_bitcast_fusion), channel_id=1, source_target_pairs={{0,4},{1,5},{2,6},{3,7},{4,0},{5,1},{6,2},{7,3},{8,12},{9,13},{10,... | collective-permute-start | bytes 221192 | tf_op jit(solution)/shard_map/ppermute | solution.py:48
  13.0 3.4 %collective-permute-done.1 = bf16[9,2,8,256]{3,0,2,1:T(8,128)(2,1)S(1)} collective-permute-done((bf16[9,2,8,256]{3,0,2,1:T(8,128)(2,1)S(1)}, bf16[9,2,8,256]{3,0,2,1:T(8,128)(2,1)S(1)}, u32[]{:S(2)}, u32[]{:S(2)}) %collective-permute-start.1) | collective-permute-done | bytes 73760 | tf_op jit(solution)/shard_map/ppermute | solution.py:48
  16.5 0.0 copy-start.3
  16.5 14.5 %exchange.2 = bf16[32,32,256]{2,1,0:T(8,128)(2,1)S(1)} custom-call(bf16[32,32,256]{2,1,0:T(8,128)(2,1)S(1)} %bitcast.70), custom_call_target="tpu_custom_call" | custom-call | flops 10000000000 | bytes 1000000 | tf_op jit(solution)/shard_map/exchange/pallas_call | solution.py:371
  31.1 7.3 %collective-permute-start.4 = (bf16[9,4,8,256]{3,0,2,1:T(8,128)(2,1)S(1)}, bf16[9,4,8,256]{3,0,2,1:T(8,128)(2,1)S(1)}, u32[]{:S(2)}, u32[]{:S(2)}) collective-permute-start(bf16[9,4,8,256]{3,0,2,1:T(8,128)(2,1)S(1)} %bitcast.88), channel_id=1, source_target_pairs={{0,24},{1,25},{2,26},{3,27},{4,28},{5,29},{6,30},{7,31},{8,0},{9,1... | collective-permute-start | bytes 442376 | tf_op jit(solution)/shard_map/ppermute | solution.py:48
  38.4 0.6 collective-permute-start.3
  38.9 0.1 collective-permute-start.2
  39.0 1.9 %collective-permute-start.5 = (bf16[9,2,8,256]{3,0,2,1:T(8,128)(2,1)S(1)}, bf16[9,2,8,256]{3,0,2,1:T(8,128)(2,1)S(1)}, u32[]{:S(2)}, u32[]{:S(2)}) collective-permute-start(bf16[9,2,8,256]{3,0,2,1:T(8,128)(2,1)S(1)} %fusion.2), channel_id=1, source_target_pairs={{0,4},{1,5},{2,6},{3,7},{4,0},{5,1},{6,2},{7,3},{8,12},{9,13},{10,... | collective-permute-start | bytes 221192 | tf_op jit(solution)/shard_map/ppermute | solution.py:48
  40.9 32.5 %pool_first.1.refs_2_ = bf16[8,1024,256]{2,1,0:T(8,128)(2,1)S(1)} custom-call(s32[128,128]{1,0:T(8,128)S(1)} %bitcast.73, s32[128]{0:T(128)S(1)} %and_select_fusion.window_ref, s32[1]{0:T(128)S(6)} %copy.59.count_ref, s32[128,128]{1,0:T(8,128)S(1)} %fusion.6.slot_ref, bf16[1024,256]{1,0:T(8,128)(2,1)S(1)} %copy-done.1, bf16[1024,256]{1,0:T(8,128)(2,1)S(1)} %bitcast.77), custom_call_target="tpu_custom_call" | custom-call | flops 20000000000 | bytes 4000000 | tf_op jit(solution)/shard_map/pool_first/pallas_call | solution.py:319
  73.4 1.9 %copy-done.6 = bf16[8,1024,256]{2,1,0:T(8,128)(2,1)} copy-done((bf16[8,1024,256]{2,1,0:T(8,128)(2,1)}, bf16[8,1024,256]{2,1,0:T(8,128)(2,1)S(1)}, u32[]{:S(2)}) %copy-start.6) | copy-done | bytes 4194328
  75.3 0.1 copy.33
  75.4 0.1 stack.65
  75.5 0.1 copy_dynamic-update-slice_fusion.5
  75.5 0.1 copy_dynamic-update-slice_fusion.4
  75.6 0.1 copy_dynamic-update-slice_fusion.3
  75.7 0.1 collective-permute-start.6
  75.8 1.9 %collective-permute-done.6 = bf16[9,16,8,256]{3,2,1,0:T(8,128)(2,1)S(1)} collective-permute-done((bf16[9,16,8,256]{3,2,1,0:T(8,128)(2,1)S(1)}, bf16[9,16,8,256]{3,2,1,0:T(8,128)(2,1)S(1)}, u32[]{:S(2)}, u32[]{:S(2)}) %collective-permute-start.6) | collective-permute-done | bytes 589856 | tf_op jit(solution)/shard_map/ppermute | solution.py:48
  77.7 0.1 select_bitcast_fusion.3
  77.8 0.1 pad_maximum_fusion
  78.0 0.1 copy.37
  78.1 1.9 %copy-done.7 = bf16[8,1024,256]{2,1,0:T(8,128)(2,1)S(1)} copy-done((bf16[8,1024,256]{2,1,0:T(8,128)(2,1)S(1)}, bf16[8,1024,256]{2,1,0:T(8,128)(2,1)}, u32[]{:S(2)}) %copy-start.7) | copy-done | bytes 4194328
  80.0 4.0 %dense_first.1 = (bf16[1024,256]{1,0:T(8,128)(2,1)S(1)}, bf16[1024,256]{1,0:T(8,128)(2,1)S(1)}) custom-call(s32[32,32]{1,0:T(8,128)S(1)} %bitcast.72, bf16[1024,256]{1,0:T(8,128)(2,1)S(1)} %copy-done.1, bf16[8,1024,256]{2,1,0:T(8,128)(2,1)S(1)} %copy-done.7, bf16[9,256,256]{2,1,0:T(8,128)(2,1)S(1)} %bitcast.68, f32[1,256]{1,0:T(1,128)S(1)} %bitcast.75), custom_call_target="tpu_custom_call" | custom-call | flops 3000000000 | bytes 6000000 | tf_op jit(solution)/shard_map/dense_first/pallas_call | solution.py:352
  84.0 14.9 %exchange.3 = bf16[32,32,256]{2,1,0:T(8,128)(2,1)S(1)} custom-call(bf16[32,32,256]{2,1,0:T(8,128)(2,1)S(1)} %bitcast.79), custom_call_target="tpu_custom_call" | custom-call | flops 10000000000 | bytes 1000000 | tf_op jit(solution)/shard_map/exchange/pallas_call | solution.py:371
  98.9 7.3 %collective-permute-start.9 = (bf16[9,4,8,256]{3,0,2,1:T(8,128)(2,1)S(1)}, bf16[9,4,8,256]{3,0,2,1:T(8,128)(2,1)S(1)}, u32[]{:S(2)}, u32[]{:S(2)}) collective-permute-start(bf16[9,4,8,256]{3,0,2,1:T(8,128)(2,1)S(1)} %bitcast.84), channel_id=1, source_target_pairs={{0,24},{1,25},{2,26},{3,27},{4,28},{5,29},{6,30},{7,31},{8,0},{9,1... | collective-permute-start | bytes 442376 | tf_op jit(solution)/shard_map/ppermute | solution.py:48
  106.2 0.6 collective-permute-start.8
  106.8 0.1 collective-permute-start.7
  106.8 32.5 %pool_second.1.refs_1_ = bf16[8,1024,256]{2,1,0:T(8,128)(2,1)S(1)} custom-call(s32[128,128]{1,0:T(8,128)S(1)} %bitcast.74, s32[128]{0:T(128)S(1)} %and_select_fusion.window_ref, s32[1]{0:T(128)S(6)} %copy.59.count_ref, s32[128,128]{1,0:T(8,128)S(1)} %fusion.6.slot_ref, bf16[1024,256]{1,0:T(8,128)(2,1)S(1)} %get-tuple-element.34.own_ref.refs_0_, ...), custom_call_target="tpu_custom_call" | custom-call | flops 20000000000 | bytes 4000000 | tf_op jit(solution)/shard_map/pool_second/pallas_call | solution.py:319
  139.3 0.1 copy.38
  139.4 0.1 stack.72
  139.5 0.1 copy_dynamic-update-slice_fusion.2
  139.5 0.1 copy_dynamic-update-slice_fusion.1
  139.6 0.1 copy_dynamic-update-slice_fusion
  139.7 0.1 collective-permute-start.10
  139.7 2.0 %collective-permute-done.10 = bf16[9,16,8,256]{3,2,1,0:T(8,128)(2,1)S(1)} collective-permute-done((bf16[9,16,8,256]{3,2,1,0:T(8,128)(2,1)S(1)}, bf16[9,16,8,256]{3,2,1,0:T(8,128)(2,1)S(1)}, u32[]{:S(2)}, u32[]{:S(2)}) %collective-permute-start.10) | collective-permute-done | bytes 589856 | tf_op jit(solution)/shard_map/ppermute | solution.py:48
  141.7 0.1 select_bitcast_fusion.1
  141.9 0.0 copy-start.5
  141.9 0.1 pad_maximum_fusion.1
  142.0 0.6 copy-done.5
  142.6 2.7 %dense_second.1 = bf16[1024,256]{1,0:T(8,128)(2,1)} custom-call(bf16[1024,256]{1,0:T(8,128)(2,1)S(1)} %get-tuple-element.34.own_ref.refs_0_, bf16[8,1024,256]{2,1,0:T(8,128)(2,1)S(1)} %pool_second.1.refs_1_, bf16[9,256,256]{2,1,0:T(8,128)(2,1)S(1)} %bitcast.69, f32[1,256]{1,0:T(1,128)S(1)} %bitcast.76), custom_call_target="tpu_custom_call" | custom-call | flops 3000000000 | bytes 6000000 | tf_op jit(solution)/shard_map/dense_second/pallas_call | solution.py:352
  (29 shorter events, 0.3 us)
Async XLA Ops:
  0.0 1.5 %copy-start = (bf16[30,8,256]{2,1,0:T(8,128)(2,1)S(1)}, bf16[30,8,256]{2,1,0:T(8,128)(2,1)}, u32[]{:S(2)}) copy-start(bf16[30,8,256]{2,1,0:T(8,128)(2,1)} %param.20) | copy-start | bytes 368644
  0.0 9.2 %copy-start.1 = (bf16[1024,256]{1,0:T(8,128)(2,1)S(1)}, bf16[1024,256]{1,0:T(8,128)(2,1)}, u32[]{:S(2)}) copy-start(bf16[1024,256]{1,0:T(8,128)(2,1)} %refs_1_.1) | copy-start | bytes 1572868
  0.0 9.2 %copy-start.2 = (s32[1,32,32]{2,1,0:T(8,128)S(1)}, s32[1,32,32]{2,1,0:T(8,128)}, u32[]{:S(2)}) copy-start(s32[1,32,32]{2,1,0:T(8,128)} %param.19) | copy-start | bytes 12292
  3.5 7.8 %collective-permute-start = (bf16[18,1,8,256]{3,0,2,1:T(8,128)(2,1)S(1)}, bf16[18,1,8,256]{3,0,2,1:T(8,128)(2,1)S(1)}, u32[]{:S(2)}, u32[]{:S(2)}) collective-permute-start(bf16[18,1,8,256]{3,0,2,1:T(8,128)(2,1)S(1)} %pad_maximum_fusion.5), channel_id=1, source_target_pairs={{0,2},{1,3},{2,0},{3,1},{4,6},{5,7},{6,4},{7,5},{8,10},{9,11},{10,... | collective-permute-start | bytes 221192 | tf_op jit(solution)/shard_map/ppermute | solution.py:48
  11.4 5.0 %collective-permute-start.1 = (bf16[9,2,8,256]{3,0,2,1:T(8,128)(2,1)S(1)}, bf16[9,2,8,256]{3,0,2,1:T(8,128)(2,1)S(1)}, u32[]{:S(2)}, u32[]{:S(2)}) collective-permute-start(bf16[9,2,8,256]{3,0,2,1:T(8,128)(2,1)S(1)} %slice_bitcast_fusion), channel_id=1, source_target_pairs={{0,4},{1,5},{2,6},{3,7},{4,0},{5,1},{6,2},{7,3},{8,12},{9,13},{10,... | collective-permute-start | bytes 221192 | tf_op jit(solution)/shard_map/ppermute | solution.py:48
  16.5 24.4 %copy-start.3 = (s32[1,128,128]{2,1,0:T(8,128)S(1)}, s32[1,128,128]{2,1,0:T(8,128)}, u32[]{:S(2)}) copy-start(s32[1,128,128]{2,1,0:T(8,128)} %param.15) | copy-start | bytes 196612
  31.1 44.3 %collective-permute-start.4 = (bf16[9,4,8,256]{3,0,2,1:T(8,128)(2,1)S(1)}, bf16[9,4,8,256]{3,0,2,1:T(8,128)(2,1)S(1)}, u32[]{:S(2)}, u32[]{:S(2)}) collective-permute-start(bf16[9,4,8,256]{3,0,2,1:T(8,128)(2,1)S(1)} %bitcast.88), channel_id=1, source_target_pairs={{0,24},{1,25},{2,26},{3,27},{4,28},{5,29},{6,30},{7,31},{8,0},{9,1... | collective-permute-start | bytes 442376 | tf_op jit(solution)/shard_map/ppermute | solution.py:48
  38.4 37.0 %collective-permute-start.3 = (bf16[9,4,8,256]{3,0,2,1:T(8,128)(2,1)S(1)}, bf16[9,4,8,256]{3,0,2,1:T(8,128)(2,1)S(1)}, u32[]{:S(2)}, u32[]{:S(2)}) collective-permute-start(bf16[9,4,8,256]{3,0,2,1:T(8,128)(2,1)S(1)} %bitcast.89), channel_id=1, source_target_pairs={{0,16},{1,17},{2,18},{3,19},{4,20},{5,21},{6,22},{7,23},{8,24},{9,... | collective-permute-start | bytes 442376 | tf_op jit(solution)/shard_map/ppermute | solution.py:48
  38.9 36.4 %collective-permute-start.2 = (bf16[9,4,8,256]{3,0,2,1:T(8,128)(2,1)S(1)}, bf16[9,4,8,256]{3,0,2,1:T(8,128)(2,1)S(1)}, u32[]{:S(2)}, u32[]{:S(2)}) collective-permute-start(bf16[9,4,8,256]{3,0,2,1:T(8,128)(2,1)S(1)} %bitcast.90), channel_id=1, source_target_pairs={{0,8},{1,9},{2,10},{3,11},{4,12},{5,13},{6,14},{7,15},{8,16},{9,17... | collective-permute-start | bytes 442376 | tf_op jit(solution)/shard_map/ppermute | solution.py:48
  39.0 36.3 %collective-permute-start.5 = (bf16[9,2,8,256]{3,0,2,1:T(8,128)(2,1)S(1)}, bf16[9,2,8,256]{3,0,2,1:T(8,128)(2,1)S(1)}, u32[]{:S(2)}, u32[]{:S(2)}) collective-permute-start(bf16[9,2,8,256]{3,0,2,1:T(8,128)(2,1)S(1)} %fusion.2), channel_id=1, source_target_pairs={{0,4},{1,5},{2,6},{3,7},{4,0},{5,1},{6,2},{7,3},{8,12},{9,13},{10,... | collective-permute-start | bytes 221192 | tf_op jit(solution)/shard_map/ppermute | solution.py:48
  73.4 1.9 %copy-start.6 = (bf16[8,1024,256]{2,1,0:T(8,128)(2,1)}, bf16[8,1024,256]{2,1,0:T(8,128)(2,1)S(1)}, u32[]{:S(2)}) copy-start(bf16[8,1024,256]{2,1,0:T(8,128)(2,1)S(1)} %pool_first.1.refs_2_) | copy-start | bytes 12582916
  75.7 2.1 %collective-permute-start.6 = (bf16[9,16,8,256]{3,2,1,0:T(8,128)(2,1)S(1)}, bf16[9,16,8,256]{3,2,1,0:T(8,128)(2,1)S(1)}, u32[]{:S(2)}, u32[]{:S(2)}) collective-permute-start(bf16[9,16,8,256]{3,2,1,0:T(8,128)(2,1)S(1)} %bitcast.82), channel_id=1, source_target_pairs={{0,1},{1,0},{2,3},{3,2},{4,5},{5,4},{6,7},{7,6},{8,9},{9,8},{10,11... | collective-permute-start | bytes 1769480 | tf_op jit(solution)/shard_map/ppermute | solution.py:48
  77.8 2.2 %copy-start.7 = (bf16[8,1024,256]{2,1,0:T(8,128)(2,1)S(1)}, bf16[8,1024,256]{2,1,0:T(8,128)(2,1)}, u32[]{:S(2)}) copy-start(bf16[8,1024,256]{2,1,0:T(8,128)(2,1)} %copy-done.6) | copy-start | bytes 12582916
  77.9 2.1 %copy-start.4 = (f32[256]{0:T(256)S(1)}, f32[256]{0:T(256)}, u32[]{:S(2)}) copy-start(f32[256]{0:T(256)} %param.23) | copy-start | bytes 3076
  98.9 40.5 %collective-permute-start.9 = (bf16[9,4,8,256]{3,0,2,1:T(8,128)(2,1)S(1)}, bf16[9,4,8,256]{3,0,2,1:T(8,128)(2,1)S(1)}, u32[]{:S(2)}, u32[]{:S(2)}) collective-permute-start(bf16[9,4,8,256]{3,0,2,1:T(8,128)(2,1)S(1)} %bitcast.84), channel_id=1, source_target_pairs={{0,24},{1,25},{2,26},{3,27},{4,28},{5,29},{6,30},{7,31},{8,0},{9,1... | collective-permute-start | bytes 442376 | tf_op jit(solution)/shard_map/ppermute | solution.py:48
  106.2 33.2 %collective-permute-start.8 = (bf16[9,4,8,256]{3,0,2,1:T(8,128)(2,1)S(1)}, bf16[9,4,8,256]{3,0,2,1:T(8,128)(2,1)S(1)}, u32[]{:S(2)}, u32[]{:S(2)}) collective-permute-start(bf16[9,4,8,256]{3,0,2,1:T(8,128)(2,1)S(1)} %bitcast.85), channel_id=1, source_target_pairs={{0,16},{1,17},{2,18},{3,19},{4,20},{5,21},{6,22},{7,23},{8,24},{9,... | collective-permute-start | bytes 442376 | tf_op jit(solution)/shard_map/ppermute | solution.py:48
  106.8 32.6 %collective-permute-start.7 = (bf16[9,4,8,256]{3,0,2,1:T(8,128)(2,1)S(1)}, bf16[9,4,8,256]{3,0,2,1:T(8,128)(2,1)S(1)}, u32[]{:S(2)}, u32[]{:S(2)}) collective-permute-start(bf16[9,4,8,256]{3,0,2,1:T(8,128)(2,1)S(1)} %bitcast.86), channel_id=1, source_target_pairs={{0,8},{1,9},{2,10},{3,11},{4,12},{5,13},{6,14},{7,15},{8,16},{9,17... | collective-permute-start | bytes 442376 | tf_op jit(solution)/shard_map/ppermute | solution.py:48
  139.7 2.1 %collective-permute-start.10 = (bf16[9,16,8,256]{3,2,1,0:T(8,128)(2,1)S(1)}, bf16[9,16,8,256]{3,2,1,0:T(8,128)(2,1)S(1)}, u32[]{:S(2)}, u32[]{:S(2)}) collective-permute-start(bf16[9,16,8,256]{3,2,1,0:T(8,128)(2,1)S(1)} %bitcast.80), channel_id=1, source_target_pairs={{0,1},{1,0},{2,3},{3,2},{4,5},{5,4},{6,7},{7,6},{8,9},{9,8},{10,11... | collective-permute-start | bytes 1769480 | tf_op jit(solution)/shard_map/ppermute | solution.py:48
  141.9 0.7 copy-start.5

commit v2 on v1

--- a/solution.py
+++ b/solution.py
@@ -89,10 +89,11 @@
 
 
 def pick_rows(list_ref, major, minor, count, table_ref, held_ref, parts):
+    listed = list_ref.at[major]
     for row in range(count):
-        source = list_ref[major, minor + row]
+        source = listed[minor + row]
         held_ref[pl.ds(row * parts, parts), :] = table_ref[
-            pl.ds(pl.multiple_of(source * parts, parts), parts), :
+            pl.ds(pl.multiple_of(source, parts), parts), :
         ]
 
 
@@ -407,8 +408,9 @@
     targets = edge_target[0]
     windows = targets[:, 0] // WIN
     local_slot = edge_relation[0] * WIN + targets % WIN
-    edges = (edge_source[0], windows, block_count, local_slot)
-    send_rows = send_list[0]
+    lanes = features.shape[1] // 128
+    edges = (edge_source[0] * lanes, windows, block_count, local_slot)
+    send_rows = send_list[0] * lanes
     peers = send_rows.shape[0]
     relations = coef_first.shape[0]
     width = features.shape[1]

time: 147 us -> 133 us (0.905)
  Pallas kernels: 103 us -> 88.3 us
  other arithmetic: 1.68 us -> 3.23 us
    pallas_call x2, Pallas kernels: 64.9 us -> 49.6 us  [pooled_means(): pl.pallas_call(pool_kernel, out_shape=jax.ShapeDtypeStruct((relations, no...]
    mul x0 -> x2, other arithmetic: none -> 1.57 us  [the longest x1 0.84 us: shards(): edges = (edge_source[0] * lanes, windows, block_count, local_slot)]
    unnamed x16 -> x12, local copies, waits for them, and re-layouts: 4.46 us -> 4.46 us
  transfers between devices with their start and end apart: 11 -> 11, of which waited for: 3 -> 3; matrix products, arithmetic and copies ran while one was open for 1% -> 3% of each run, Pallas kernels for 46% -> 39%
where the time goes in v2:
time: 133 us; the launch traced here: 132 us
  Pallas kernels  88.3 us (66%)
  starting transfers between devices  22.5 us (17%)
  local copies, waits for them, and re-layouts  7.53 us (6%)
  waiting for transfers between devices  7.32 us (6%)
  other arithmetic  3.23 us (2%)
  matrix products  1.95 us (1%)
    pallas_call x2, Pallas kernels, pooled_means(): pl.pallas_call(pool_kernel, out_shape=jax.ShapeDtypeStruct((relations, no...  49.6 us
    pallas_call x2, Pallas kernels, exchange(): pl.pallas_call(functools.partial(exchange_kernel, peers), out_shape=jax.S...  30.3 us
    ppermute x11, starting transfers between devices, send_digit(): lax.ppermute(share, 'dom', shift_pairs(devices, radix, stride, hop))  22.5 us
    ppermute x11, waiting for transfers between devices, send_digit(): lax.ppermute(share, 'dom', shift_pairs(devices, radix, stride, hop))  7.32 us
    pallas_call x2, Pallas kernels, dense_rows(): pl.pallas_call(functools.partial(dense_kernel, last), out_shape=result if...  6.44 us
    unnamed x12, local copies, waits for them, and re-layouts  4.46 us
  transfers between devices with their start and end apart: 11, of which 3 were waited for; matrix products, arithmetic and copies ran while one was open for 3% of the time, Pallas kernels for 39%

profile of v2, /device:TPU:0, one launch (start us, length us, event | category | flops | bytes accessed | tf_op | source)
XLA Modules:
  0.0 132.0 jit_solution(2569811317506981993)
XLA Ops:
  0.0 0.8 copy.29
  0.8 0.7 copy.31
  1.5 0.9 convolution_convert_fusion.1
  2.3 1.1 convolution_convert_fusion
  3.5 3.0 %collective-permute-start = (bf16[18,1,8,256]{3,0,2,1:T(8,128)(2,1)S(1)}, bf16[18,1,8,256]{3,0,2,1:T(8,128)(2,1)S(1)}, u32[]{:S(2)}, u32[]{:S(2)}) collective-permute-start(bf16[18,1,8,256]{3,0,2,1:T(8,128)(2,1)S(1)} %pad_maximum_fusion.5), channel_id=1, source_target_pairs={{0,2},{1,3},{2,0},{3,1},{4,6},{5,7},{6,4},{7,5},{8,10},{9,11},{10,... | collective-permute-start | bytes 221192 | tf_op jit(solution)/shard_map/ppermute | solution.py:48
  6.5 0.9 slice_reduce_fusion
  7.5 0.7 multiply_bitcast_fusion.1.send_ref.refs_0_
  8.2 0.8 multiply_bitcast_fusion.source_ref
  9.0 0.9 fusion.6.slot_ref
  10.7 1.9 %outgoing.1 = bf16[1024,256]{1,0:T(8,128)(2,1)S(1)} custom-call(s32[32,32]{1,0:T(8,128)S(1)} %multiply_bitcast_fusion.1.send_ref.refs_0_, bf16[1024,256]{1,0:T(8,128)(2,1)S(1)} %copy-done.1), custom_call_target="tpu_custom_call" | custom-call | tf_op jit(solution)/shard_map/outgoing/pallas_call | solution.py:297
  12.6 0.1 select_bitcast_fusion.9
  12.7 1.6 %collective-permute-start.1 = (bf16[9,2,8,256]{3,0,2,1:T(8,128)(2,1)S(1)}, bf16[9,2,8,256]{3,0,2,1:T(8,128)(2,1)S(1)}, u32[]{:S(2)}, u32[]{:S(2)}) collective-permute-start(bf16[9,2,8,256]{3,0,2,1:T(8,128)(2,1)S(1)} %slice_bitcast_fusion), channel_id=1, source_target_pairs={{0,4},{1,5},{2,6},{3,7},{4,0},{5,1},{6,2},{7,3},{8,12},{9,13},{10,... | collective-permute-start | bytes 221192 | tf_op jit(solution)/shard_map/ppermute | solution.py:48
  14.4 3.4 %collective-permute-done.1 = bf16[9,2,8,256]{3,0,2,1:T(8,128)(2,1)S(1)} collective-permute-done((bf16[9,2,8,256]{3,0,2,1:T(8,128)(2,1)S(1)}, bf16[9,2,8,256]{3,0,2,1:T(8,128)(2,1)S(1)}, u32[]{:S(2)}, u32[]{:S(2)}) %collective-permute-start.1) | collective-permute-done | bytes 73760 | tf_op jit(solution)/shard_map/ppermute | solution.py:48
  17.8 14.5 %exchange.2 = bf16[32,32,256]{2,1,0:T(8,128)(2,1)S(1)} custom-call(bf16[32,32,256]{2,1,0:T(8,128)(2,1)S(1)} %bitcast.72), custom_call_target="tpu_custom_call" | custom-call | flops 10000000000 | bytes 1000000 | tf_op jit(solution)/shard_map/exchange/pallas_call | solution.py:372
  32.4 7.3 %collective-permute-start.4 = (bf16[9,4,8,256]{3,0,2,1:T(8,128)(2,1)S(1)}, bf16[9,4,8,256]{3,0,2,1:T(8,128)(2,1)S(1)}, u32[]{:S(2)}, u32[]{:S(2)}) collective-permute-start(bf16[9,4,8,256]{3,0,2,1:T(8,128)(2,1)S(1)} %bitcast.86), channel_id=1, source_target_pairs={{0,24},{1,25},{2,26},{3,27},{4,28},{5,29},{6,30},{7,31},{8,0},{9,1... | collective-permute-start | bytes 442376 | tf_op jit(solution)/shard_map/ppermute | solution.py:48
  39.7 0.6 collective-permute-start.3
  40.3 0.1 collective-permute-start.2
  40.3 1.9 %collective-permute-start.5 = (bf16[9,2,8,256]{3,0,2,1:T(8,128)(2,1)S(1)}, bf16[9,2,8,256]{3,0,2,1:T(8,128)(2,1)S(1)}, u32[]{:S(2)}, u32[]{:S(2)}) collective-permute-start(bf16[9,2,8,256]{3,0,2,1:T(8,128)(2,1)S(1)} %fusion.2), channel_id=1, source_target_pairs={{0,4},{1,5},{2,6},{3,7},{4,0},{5,1},{6,2},{7,3},{8,12},{9,13},{10,... | collective-permute-start | bytes 221192 | tf_op jit(solution)/shard_map/ppermute | solution.py:48
  42.2 24.8 %pool_first.1.refs_2_ = bf16[8,1024,256]{2,1,0:T(8,128)(2,1)S(1)} custom-call(s32[128,128]{1,0:T(8,128)S(1)} %multiply_bitcast_fusion.source_ref, s32[128]{0:T(128)S(1)} %and_select_fusion.window_ref, s32[1]{0:T(128)S(6)} %copy.59.count_ref, s32[128,128]{1,0:T(8,128)S(1)} %fusion.6.slot_ref, bf16[1024,256]{1,0:T(8,128)(2,1)S(1)} %copy-done.1, ...), custom_call_target="tpu_custom_call" | custom-call | flops 20000000000 | bytes 4000000 | tf_op jit(solution)/shard_map/pool_first/pallas_call | solution.py:320
  67.0 1.9 %copy-done.4 = bf16[8,1024,256]{2,1,0:T(8,128)(2,1)} copy-done((bf16[8,1024,256]{2,1,0:T(8,128)(2,1)}, bf16[8,1024,256]{2,1,0:T(8,128)(2,1)S(1)}, u32[]{:S(2)}) %copy-start.4) | copy-done | bytes 4194328
  69.0 0.1 copy.33
  69.1 0.1 stack.65
  69.1 0.1 copy_dynamic-update-slice_fusion.5
  69.2 0.1 copy_dynamic-update-slice_fusion.4
  69.3 0.1 copy_dynamic-update-slice_fusion.3
  69.3 0.1 collective-permute-start.6
  69.5 1.9 %collective-permute-done.6 = bf16[9,16,8,256]{3,2,1,0:T(8,128)(2,1)S(1)} collective-permute-done((bf16[9,16,8,256]{3,2,1,0:T(8,128)(2,1)S(1)}, bf16[9,16,8,256]{3,2,1,0:T(8,128)(2,1)S(1)}, u32[]{:S(2)}, u32[]{:S(2)}) %collective-permute-start.6) | collective-permute-done | bytes 589856 | tf_op jit(solution)/shard_map/ppermute | solution.py:48
  71.4 0.1 select_bitcast_fusion.3
  71.5 0.1 pad_maximum_fusion
  71.6 0.1 copy.37
  71.7 1.9 %copy-done.5 = bf16[8,1024,256]{2,1,0:T(8,128)(2,1)S(1)} copy-done((bf16[8,1024,256]{2,1,0:T(8,128)(2,1)S(1)}, bf16[8,1024,256]{2,1,0:T(8,128)(2,1)}, u32[]{:S(2)}) %copy-start.5) | copy-done | bytes 4194328
  73.7 3.7 %dense_first.1 = (bf16[1024,256]{1,0:T(8,128)(2,1)S(1)}, bf16[1024,256]{1,0:T(8,128)(2,1)S(1)}) custom-call(s32[32,32]{1,0:T(8,128)S(1)} %multiply_bitcast_fusion.1.send_ref.refs_0_, bf16[1024,256]{1,0:T(8,128)(2,1)S(1)} %copy-done.1, bf16[8,1024,256]{2,1,0:T(8,128)(2,1)S(1)} %copy-done.5, bf16[9,256,256]{2,1,0:T(8,128)(2,1)S(1)} %bitcast.70, ...), custom_call_target="tpu_custom_call" | custom-call | flops 3000000000 | bytes 6000000 | tf_op jit(solution)/shard_map/dense_first/pallas_call | solution.py:353
  77.4 15.8 %exchange.3 = bf16[32,32,256]{2,1,0:T(8,128)(2,1)S(1)} custom-call(bf16[32,32,256]{2,1,0:T(8,128)(2,1)S(1)} %bitcast.77), custom_call_target="tpu_custom_call" | custom-call | flops 10000000000 | bytes 1000000 | tf_op jit(solution)/shard_map/exchange/pallas_call | solution.py:372
  93.2 7.3 %collective-permute-start.9 = (bf16[9,4,8,256]{3,0,2,1:T(8,128)(2,1)S(1)}, bf16[9,4,8,256]{3,0,2,1:T(8,128)(2,1)S(1)}, u32[]{:S(2)}, u32[]{:S(2)}) collective-permute-start(bf16[9,4,8,256]{3,0,2,1:T(8,128)(2,1)S(1)} %bitcast.82), channel_id=1, source_target_pairs={{0,24},{1,25},{2,26},{3,27},{4,28},{5,29},{6,30},{7,31},{8,0},{9,1... | collective-permute-start | bytes 442376 | tf_op jit(solution)/shard_map/ppermute | solution.py:48
  100.5 0.6 collective-permute-start.8
  101.1 0.1 collective-permute-start.7
  101.2 24.8 %pool_second.1.refs_1_ = bf16[8,1024,256]{2,1,0:T(8,128)(2,1)S(1)} custom-call(s32[128,128]{1,0:T(8,128)S(1)} %multiply_bitcast_fusion.source_ref, s32[128]{0:T(128)S(1)} %and_select_fusion.window_ref, s32[1]{0:T(128)S(6)} %copy.59.count_ref, s32[128,128]{1,0:T(8,128)S(1)} %fusion.6.slot_ref, bf16[1024,256]{1,0:T(8,128)(2,1)S(1)} %get-tuple-element.34.own_ref.refs_0_, ...), custom_call_target="tpu_custom_call" | custom-call | flops 20000000000 | bytes 4000000 | tf_op jit(solution)/shard_map/pool_second/pallas_call | solution.py:320
  126.0 0.1 copy.38
  126.1 0.1 stack.72
  126.2 0.1 copy_dynamic-update-slice_fusion.2
  126.2 0.1 copy_dynamic-update-slice_fusion.1
  126.3 0.1 copy_dynamic-update-slice_fusion
  126.4 0.1 collective-permute-start.10
  126.4 2.0 %collective-permute-done.10 = bf16[9,16,8,256]{3,2,1,0:T(8,128)(2,1)S(1)} collective-permute-done((bf16[9,16,8,256]{3,2,1,0:T(8,128)(2,1)S(1)}, bf16[9,16,8,256]{3,2,1,0:T(8,128)(2,1)S(1)}, u32[]{:S(2)}, u32[]{:S(2)}) %collective-permute-start.10) | collective-permute-done | bytes 589856 | tf_op jit(solution)/shard_map/ppermute | solution.py:48
  128.4 0.1 select_bitcast_fusion.1
  128.6 0.1 pad_maximum_fusion.1
  128.7 0.6 copy-done.3
  129.3 2.7 %dense_second.1 = bf16[1024,256]{1,0:T(8,128)(2,1)} custom-call(bf16[1024,256]{1,0:T(8,128)(2,1)S(1)} %get-tuple-element.34.own_ref.refs_0_, bf16[8,1024,256]{2,1,0:T(8,128)(2,1)S(1)} %pool_second.1.refs_1_, bf16[9,256,256]{2,1,0:T(8,128)(2,1)S(1)} %bitcast.71, f32[1,256]{1,0:T(1,128)S(1)} %bitcast.74), custom_call_target="tpu_custom_call" | custom-call | flops 3000000000 | bytes 6000000 | tf_op jit(solution)/shard_map/dense_second/pallas_call | solution.py:353
  (27 shorter events, 0.3 us)
Async XLA Ops:
  0.0 1.5 %copy-start = (bf16[30,8,256]{2,1,0:T(8,128)(2,1)S(1)}, bf16[30,8,256]{2,1,0:T(8,128)(2,1)}, u32[]{:S(2)}) copy-start(bf16[30,8,256]{2,1,0:T(8,128)(2,1)} %param.20) | copy-start | bytes 368644
  0.0 10.7 %copy-start.1 = (bf16[1024,256]{1,0:T(8,128)(2,1)S(1)}, bf16[1024,256]{1,0:T(8,128)(2,1)}, u32[]{:S(2)}) copy-start(bf16[1024,256]{1,0:T(8,128)(2,1)} %refs_1_.1) | copy-start | bytes 1572868
  3.5 9.1 %collective-permute-start = (bf16[18,1,8,256]{3,0,2,1:T(8,128)(2,1)S(1)}, bf16[18,1,8,256]{3,0,2,1:T(8,128)(2,1)S(1)}, u32[]{:S(2)}, u32[]{:S(2)}) collective-permute-start(bf16[18,1,8,256]{3,0,2,1:T(8,128)(2,1)S(1)} %pad_maximum_fusion.5), channel_id=1, source_target_pairs={{0,2},{1,3},{2,0},{3,1},{4,6},{5,7},{6,4},{7,5},{8,10},{9,11},{10,... | collective-permute-start | bytes 221192 | tf_op jit(solution)/shard_map/ppermute | solution.py:48
  12.7 5.0 %collective-permute-start.1 = (bf16[9,2,8,256]{3,0,2,1:T(8,128)(2,1)S(1)}, bf16[9,2,8,256]{3,0,2,1:T(8,128)(2,1)S(1)}, u32[]{:S(2)}, u32[]{:S(2)}) collective-permute-start(bf16[9,2,8,256]{3,0,2,1:T(8,128)(2,1)S(1)} %slice_bitcast_fusion), channel_id=1, source_target_pairs={{0,4},{1,5},{2,6},{3,7},{4,0},{5,1},{6,2},{7,3},{8,12},{9,13},{10,... | collective-permute-start | bytes 221192 | tf_op jit(solution)/shard_map/ppermute | solution.py:48
  32.4 36.7 %collective-permute-start.4 = (bf16[9,4,8,256]{3,0,2,1:T(8,128)(2,1)S(1)}, bf16[9,4,8,256]{3,0,2,1:T(8,128)(2,1)S(1)}, u32[]{:S(2)}, u32[]{:S(2)}) collective-permute-start(bf16[9,4,8,256]{3,0,2,1:T(8,128)(2,1)S(1)} %bitcast.86), channel_id=1, source_target_pairs={{0,24},{1,25},{2,26},{3,27},{4,28},{5,29},{6,30},{7,31},{8,0},{9,1... | collective-permute-start | bytes 442376 | tf_op jit(solution)/shard_map/ppermute | solution.py:48
  39.7 29.4 %collective-permute-start.3 = (bf16[9,4,8,256]{3,0,2,1:T(8,128)(2,1)S(1)}, bf16[9,4,8,256]{3,0,2,1:T(8,128)(2,1)S(1)}, u32[]{:S(2)}, u32[]{:S(2)}) collective-permute-start(bf16[9,4,8,256]{3,0,2,1:T(8,128)(2,1)S(1)} %bitcast.87), channel_id=1, source_target_pairs={{0,16},{1,17},{2,18},{3,19},{4,20},{5,21},{6,22},{7,23},{8,24},{9,... | collective-permute-start | bytes 442376 | tf_op jit(solution)/shard_map/ppermute | solution.py:48
  40.3 28.8 %collective-permute-start.2 = (bf16[9,4,8,256]{3,0,2,1:T(8,128)(2,1)S(1)}, bf16[9,4,8,256]{3,0,2,1:T(8,128)(2,1)S(1)}, u32[]{:S(2)}, u32[]{:S(2)}) collective-permute-start(bf16[9,4,8,256]{3,0,2,1:T(8,128)(2,1)S(1)} %bitcast.88), channel_id=1, source_target_pairs={{0,8},{1,9},{2,10},{3,11},{4,12},{5,13},{6,14},{7,15},{8,16},{9,17... | collective-permute-start | bytes 442376 | tf_op jit(solution)/shard_map/ppermute | solution.py:48
  40.3 28.7 %collective-permute-start.5 = (bf16[9,2,8,256]{3,0,2,1:T(8,128)(2,1)S(1)}, bf16[9,2,8,256]{3,0,2,1:T(8,128)(2,1)S(1)}, u32[]{:S(2)}, u32[]{:S(2)}) collective-permute-start(bf16[9,2,8,256]{3,0,2,1:T(8,128)(2,1)S(1)} %fusion.2), channel_id=1, source_target_pairs={{0,4},{1,5},{2,6},{3,7},{4,0},{5,1},{6,2},{7,3},{8,12},{9,13},{10,... | collective-permute-start | bytes 221192 | tf_op jit(solution)/shard_map/ppermute | solution.py:48
  67.0 1.9 %copy-start.4 = (bf16[8,1024,256]{2,1,0:T(8,128)(2,1)}, bf16[8,1024,256]{2,1,0:T(8,128)(2,1)S(1)}, u32[]{:S(2)}) copy-start(bf16[8,1024,256]{2,1,0:T(8,128)(2,1)S(1)} %pool_first.1.refs_2_) | copy-start | bytes 12582916
  69.3 2.1 %collective-permute-start.6 = (bf16[9,16,8,256]{3,2,1,0:T(8,128)(2,1)S(1)}, bf16[9,16,8,256]{3,2,1,0:T(8,128)(2,1)S(1)}, u32[]{:S(2)}, u32[]{:S(2)}) collective-permute-start(bf16[9,16,8,256]{3,2,1,0:T(8,128)(2,1)S(1)} %bitcast.80), channel_id=1, source_target_pairs={{0,1},{1,0},{2,3},{3,2},{4,5},{5,4},{6,7},{7,6},{8,9},{9,8},{10,11... | collective-permute-start | bytes 1769480 | tf_op jit(solution)/shard_map/ppermute | solution.py:48
  71.5 2.2 %copy-start.5 = (bf16[8,1024,256]{2,1,0:T(8,128)(2,1)S(1)}, bf16[8,1024,256]{2,1,0:T(8,128)(2,1)}, u32[]{:S(2)}) copy-start(bf16[8,1024,256]{2,1,0:T(8,128)(2,1)} %copy-done.4) | copy-start | bytes 12582916
  71.6 2.1 %copy-start.2 = (f32[256]{0:T(256)S(1)}, f32[256]{0:T(256)}, u32[]{:S(2)}) copy-start(f32[256]{0:T(256)} %param.23) | copy-start | bytes 3076
  93.2 32.8 %collective-permute-start.9 = (bf16[9,4,8,256]{3,0,2,1:T(8,128)(2,1)S(1)}, bf16[9,4,8,256]{3,0,2,1:T(8,128)(2,1)S(1)}, u32[]{:S(2)}, u32[]{:S(2)}) collective-permute-start(bf16[9,4,8,256]{3,0,2,1:T(8,128)(2,1)S(1)} %bitcast.82), channel_id=1, source_target_pairs={{0,24},{1,25},{2,26},{3,27},{4,28},{5,29},{6,30},{7,31},{8,0},{9,1... | collective-permute-start | bytes 442376 | tf_op jit(solution)/shard_map/ppermute | solution.py:48
  100.5 25.5 %collective-permute-start.8 = (bf16[9,4,8,256]{3,0,2,1:T(8,128)(2,1)S(1)}, bf16[9,4,8,256]{3,0,2,1:T(8,128)(2,1)S(1)}, u32[]{:S(2)}, u32[]{:S(2)}) collective-permute-start(bf16[9,4,8,256]{3,0,2,1:T(8,128)(2,1)S(1)} %bitcast.83), channel_id=1, source_target_pairs={{0,16},{1,17},{2,18},{3,19},{4,20},{5,21},{6,22},{7,23},{8,24},{9,... | collective-permute-start | bytes 442376 | tf_op jit(solution)/shard_map/ppermute | solution.py:48
  101.1 24.9 %collective-permute-start.7 = (bf16[9,4,8,256]{3,0,2,1:T(8,128)(2,1)S(1)}, bf16[9,4,8,256]{3,0,2,1:T(8,128)(2,1)S(1)}, u32[]{:S(2)}, u32[]{:S(2)}) collective-permute-start(bf16[9,4,8,256]{3,0,2,1:T(8,128)(2,1)S(1)} %bitcast.84), channel_id=1, source_target_pairs={{0,8},{1,9},{2,10},{3,11},{4,12},{5,13},{6,14},{7,15},{8,16},{9,17... | collective-permute-start | bytes 442376 | tf_op jit(solution)/shard_map/ppermute | solution.py:48
  126.4 2.1 %collective-permute-start.10 = (bf16[9,16,8,256]{3,2,1,0:T(8,128)(2,1)S(1)}, bf16[9,16,8,256]{3,2,1,0:T(8,128)(2,1)S(1)}, u32[]{:S(2)}, u32[]{:S(2)}) collective-permute-start(bf16[9,16,8,256]{3,2,1,0:T(8,128)(2,1)S(1)} %bitcast.78), channel_id=1, source_target_pairs={{0,1},{1,0},{2,3},{3,2},{4,5},{5,4},{6,7},{7,6},{8,9},{9,8},{10,11... | collective-permute-start | bytes 1769480 | tf_op jit(solution)/shard_map/ppermute | solution.py:48
  128.6 0.7 copy-start.3
